TPU v7x, 32 devices: a whole 2x2x4 slice. The times are simulated.
32 devices in a mesh: row: 4 (over y, core), col: 8 (over z, x).
Axes of the slice: x: 2, y: 2, z: 4, core: 2. Of those that a mesh axis runs over, the one named last changes fastest.
Arguments:
- matrix: float32 [16384, 16384], P('row', 'col'), may hold values from -500 to 500
Outputs:
- reduced: float32 [16384, 16384], P('row', 'col')
All inputs are finite; a program needn't handle non-finite values.
Results may differ from a plain program's by a relative error of at most 0.0003.
Values sent between devices are 32-bit elements; how exact they have to be, the bound alone decides.
A program may use at most 192 MiB of HBM per device.

v0:
```python
import jax
import jax.numpy as jnp
from jax import lax
from jax.sharding import PartitionSpec as P

REFL = 4
PANELS = 2
highest = lax.Precision.HIGHEST


def from_root(value, axis, source):
    kept = jnp.where(lax.axis_index(axis) == source, value, 0).astype(value.dtype)
    return lax.psum(kept, axis)


def product(left, right):
    return jnp.dot(left, right, precision=highest, preferred_element_type=jnp.float32)


def on_device(matrix):
    rows_local, cols_local = matrix.shape
    row_start = lax.axis_index("row") * rows_local
    col_start = lax.axis_index("col") * cols_local
    total = rows_local * lax.axis_size("row")
    positions = jnp.arange(total, dtype=jnp.int32)
    current = matrix
    for panel_index in range(PANELS):
        reflectors = jnp.zeros((total, REFL), jnp.float32)
        updates = jnp.zeros((total, REFL), jnp.float32)
        for inner_index in range(REFL):
            target = panel_index * REFL + inner_index
            owner = target // cols_local
            own_slice = current[:, target - owner * cols_local]
            reflector_rows = lax.dynamic_slice_in_dim(reflectors, row_start, rows_local, 0)
            update_block = lax.dynamic_slice_in_dim(updates, row_start, rows_local, 0)
            held = from_root(own_slice, "col", owner)
            column = (
                held
                - product(reflector_rows, updates[target])
                - product(update_block, reflectors[target])
            )
            whole = lax.all_gather(column, "row", axis=0, tiled=True)
            beneath = jnp.where(positions > target, whole, 0.0)
            leading = whole[target + 1]
            length = jnp.sqrt(jnp.sum(beneath * beneath))
            signed = jnp.where(leading >= 0.0, length, -length)
            vector = beneath + jnp.where(positions == target + 1, signed, 0.0)
            factor = 1.0 / (length * (length + jnp.abs(leading)))
            vector_cols = lax.dynamic_slice_in_dim(vector, col_start, cols_local, 0)
            against_updates = product(vector, updates)
            against_reflectors = product(vector, reflectors)
            summed = lax.psum(product(current, vector_cols), "col")
            mapped = factor * (
                summed
                - product(reflector_rows, against_updates)
                - product(update_block, against_reflectors)
            )
            vector_rows = lax.dynamic_slice_in_dim(vector, row_start, rows_local, 0)
            inner = lax.psum(jnp.sum(mapped * vector_rows), "row")
            update = lax.all_gather(
                mapped - 0.5 * factor * inner * vector_rows, "row", axis=0, tiled=True
            )
            reflectors = reflectors.at[:, inner_index].set(vector)
            updates = updates.at[:, inner_index].set(update)
        reflector_rows = lax.dynamic_slice_in_dim(reflectors, row_start, rows_local, 0)
        update_block = lax.dynamic_slice_in_dim(updates, row_start, rows_local, 0)
        reflector_cols = lax.dynamic_slice_in_dim(reflectors, col_start, cols_local, 0)
        update_cols = lax.dynamic_slice_in_dim(updates, col_start, cols_local, 0)
        current = (
            current
            - product(reflector_rows, update_cols.T)
            - product(update_block, reflector_cols.T)
        )
    return current


def solution(mesh):
    return jax.shard_map(
        on_device,
        mesh=mesh,
        in_specs=(P("row", "col"),),
        out_specs=P("row", "col"),
        check_vma=False,
    )
```

profile of v0, /device:TPU:0, one launch (start us, length us, event | category | flops | bytes accessed | tf_op | source)
XLA Modules:
  0.0 982.2 jit_solution(17959320532915637002)
XLA Ops:
  3.4 31.1 %copy.46 = f32[4096,2048]{0,1:T(8,128)} copy(f32[4096,2048]{1,0:T(8,128)} %param.33) | data formatting | bytes 67108864 | tf_op args[0]
  34.5 1.3 broadcast_select_fusion.16
  35.8 38.8 %psum.168 = f32[4096]{0:T(1024)S(1)} all-reduce(f32[4096]{0:T(1024)S(1)} %bitcast.324), channel_id=1, replica_groups=mesh['row'=4,'col'=8] {'col'}, use_global_device_ids=true, to_apply=%region_1.2 | all-reduce | flops 4096 | bytes 32768 | tf_op jit(solution)/shard_map/psum | solution.py:13
  74.7 5.2 all_gather.48
  83.8 1.9 fusion.2
  85.9 30.7 %fusion.128 = f32[1,4096]{1,0:T(1,128)S(1)} fusion(f32[2048,1]{0,1:T(1,128)S(1)} %bitcast.325, f32[4096,2048]{1,0:T(8,128)} %param.33), kind=kOutput, calls=%fused_computation.249 | convolution fusion | flops 100663296 | bytes 33579008 | tf_op jit(solution)/shard_map/dot_general | solution.py:17
  116.6 33.1 %all-reduce.9 = (f32[4096]{0:T(1024)S(1)}, f32[4096]{0:T(1024)S(1)}) all-reduce(f32[4096]{0:T(1024)S(1)} %bitcast.289, f32[4096]{0:T(1024)S(1)} %bitcast.322), channel_id=1, replica_groups=mesh['row'=4,'col'=8] {'col'}, use_global_device_ids=true, to_apply=%region_5.6 | all-reduce | flops 8192 | bytes 65536 | tf_op jit(solution)/shard_map/psum | solution.py:52
  151.1 6.3 psum.171
  158.1 5.2 all_gather.49
  164.8 5.5 all_gather.50
  174.2 1.3 convolution_bitcast_fusion.11
  175.5 1.3 convolution_bitcast_fusion.12
  176.8 30.7 %fusion.129 = f32[1,4096]{1,0:T(1,128)S(1)} fusion(f32[2048,1]{0,1:T(1,128)S(1)} %bitcast.326, f32[4096,2048]{1,0:T(8,128)} %param.33), kind=kOutput, calls=%fused_computation.250 | convolution fusion | flops 100663296 | bytes 33579008 | tf_op jit(solution)/shard_map/dot_general | solution.py:17
  207.5 33.1 %all-reduce.8 = (f32[4096]{0:T(1024)S(1)}, f32[4096]{0:T(1024)S(1)}) all-reduce(f32[4096]{0:T(1024)S(1)} %bitcast.290, f32[4096]{0:T(1024)S(1)} %bitcast.320), channel_id=1, replica_groups=mesh['row'=4,'col'=8] {'col'}, use_global_device_ids=true, to_apply=%region_11.12 | all-reduce | flops 8192 | bytes 65536 | tf_op jit(solution)/shard_map/psum | solution.py:52
  241.8 6.3 psum.174
  248.6 5.2 all_gather.51
  257.9 5.7 all_gather.52
  266.9 1.3 convolution_bitcast_fusion.9
  268.2 1.3 convolution_bitcast_fusion.10
  269.5 30.7 %fusion.130 = f32[1,4096]{1,0:T(1,128)S(1)} fusion(f32[2048,1]{0,1:T(1,128)S(1)} %bitcast.327, f32[4096,2048]{1,0:T(8,128)} %param.33), kind=kOutput, calls=%fused_computation.251 | convolution fusion | flops 100663296 | bytes 33579008 | tf_op jit(solution)/shard_map/dot_general | solution.py:17
  300.2 33.1 %all-reduce.7 = (f32[4096]{0:T(1024)S(1)}, f32[4096]{0:T(1024)S(1)}) all-reduce(f32[4096]{0:T(1024)S(1)} %bitcast.291, f32[4096]{0:T(1024)S(1)} %bitcast.318), channel_id=1, replica_groups=mesh['row'=4,'col'=8] {'col'}, use_global_device_ids=true, to_apply=%region_16.17 | all-reduce | flops 8192 | bytes 65536 | tf_op jit(solution)/shard_map/psum | solution.py:52
  334.5 6.3 psum.177
  341.3 5.2 all_gather.53
  351.4 5.5 all_gather.54
  360.2 1.3 convolution_bitcast_fusion.7
  361.5 1.3 convolution_bitcast_fusion.8
  362.8 30.7 %fusion.131 = f32[1,4096]{1,0:T(1,128)S(1)} fusion(f32[2048,1]{0,1:T(1,128)S(1)} %bitcast.328, f32[4096,2048]{1,0:T(8,128)} %param.33), kind=kOutput, calls=%fused_computation.252 | convolution fusion | flops 100663296 | bytes 33579008 | tf_op jit(solution)/shard_map/dot_general | solution.py:17
  393.5 33.0 %psum.178 = f32[4096]{0:T(1024)S(1)} all-reduce(f32[4096]{0:T(1024)S(1)} %bitcast.292), channel_id=1, replica_groups=mesh['row'=4,'col'=8] {'col'}, use_global_device_ids=true, to_apply=%region_20.21 | all-reduce | flops 4096 | bytes 32768 | tf_op jit(solution)/shard_map/psum | solution.py:52
  428.9 6.3 psum.179
  435.7 5.4 all_gather.55
  442.3 30.1 %fusion.14 = f32[4096,2048]{0,1:T(8,128)} fusion(f32[16384,4]{0,1:T(4,128)S(1)} %scatter.64, s32[]{:T(128)S(6)} %select_n.183, f32[16384,4]{0,1:T(4,128)S(1)} %scatter.65, s32[]{:T(128)S(6)} %select_n.184), kind=kOutput, calls=%fused_computation.58 | convolution fusion | flops 402653184 | bytes 33652744 | tf_op jit(solution)/shard_map/dot_general | solution.py:17
  472.4 41.2 %subtract_subtract_fusion.1 = f32[4096,2048]{0,1:T(8,128)} fusion(f32[4096,2048]{0,1:T(8,128)} %copy.46, f32[4096,2048]{0,1:T(8,128)} %fusion.14, f32[16384,4]{0,1:T(4,128)S(1)} %scatter.65, s32[]{:T(128)S(6)} %select_n.183, f32[16384,4]{0,1:T(4,128)S(1)} %scatter.64, s32[]{:T(128)S(6)} %select_n.184), kind=kOutput, calls=%fused_computation.1 | convolution fusion | flops 419430400 | bytes 100761608 | tf_op jit(solution)/shard_map/dot_general | solution.py:17
  513.7 1.3 broadcast_select_fusion.12
  515.0 33.0 %psum.180 = f32[4096]{0:T(1024)S(1)} all-reduce(f32[4096]{0:T(1024)S(1)} %bitcast.323), channel_id=1, replica_groups=mesh['row'=4,'col'=8] {'col'}, use_global_device_ids=true, to_apply=%region_23.24 | all-reduce | flops 4096 | bytes 32768 | tf_op jit(solution)/shard_map/psum | solution.py:13
  548.0 5.2 all_gather.56
  557.1 1.9 fusion.3
  559.2 21.5 %fusion.132 = f32[1,4096]{1,0:T(1,128)S(1)} fusion(f32[4096,2048]{0,1:T(8,128)} %subtract_subtract_fusion.1, f32[2048,1]{0,1:T(1,128)S(1)} %bitcast.329), kind=kOutput, calls=%fused_computation.253 | convolution fusion | flops 100663296 | bytes 33579008 | tf_op jit(solution)/shard_map/dot_general | solution.py:17
  580.7 33.1 %all-reduce.6 = (f32[4096]{0:T(1024)S(1)}, f32[4096]{0:T(1024)S(1)}) all-reduce(f32[4096]{0:T(1024)S(1)} %bitcast.285, f32[4096]{0:T(1024)S(1)} %bitcast.321), channel_id=1, replica_groups=mesh['row'=4,'col'=8] {'col'}, use_global_device_ids=true, to_apply=%region_26.27 | all-reduce | flops 8192 | bytes 65536 | tf_op jit(solution)/shard_map/psum | solution.py:52
  615.2 6.3 psum.183
  622.2 5.2 all_gather.57
  628.9 5.4 all_gather.58
  638.2 1.3 convolution_bitcast_fusion.4
  639.5 1.3 convolution_bitcast_fusion.5
  640.8 21.0 %fusion.133 = f32[1,4096]{1,0:T(1,128)S(1)} fusion(f32[4096,2048]{0,1:T(8,128)} %subtract_subtract_fusion.1, f32[2048,1]{0,1:T(1,128)S(1)} %bitcast.330), kind=kOutput, calls=%fused_computation.254 | convolution fusion | flops 100663296 | bytes 33579008 | tf_op jit(solution)/shard_map/dot_general | solution.py:17
  661.9 33.2 %all-reduce.5 = (f32[4096]{0:T(1024)S(1)}, f32[4096]{0:T(1024)S(1)}) all-reduce(f32[4096]{0:T(1024)S(1)} %bitcast.286, f32[4096]{0:T(1024)S(1)} %bitcast.319), channel_id=1, replica_groups=mesh['row'=4,'col'=8] {'col'}, use_global_device_ids=true, to_apply=%region_31.32 | all-reduce | flops 8192 | bytes 65536 | tf_op jit(solution)/shard_map/psum | solution.py:52
  696.3 6.3 psum.186
  703.2 5.2 all_gather.59
  712.4 5.3 all_gather.60
  721.0 1.3 convolution_bitcast_fusion.2
  722.3 1.3 convolution_bitcast_fusion.3
  723.6 21.0 %fusion.134 = f32[1,4096]{1,0:T(1,128)S(1)} fusion(f32[4096,2048]{0,1:T(8,128)} %subtract_subtract_fusion.1, f32[2048,1]{0,1:T(1,128)S(1)} %bitcast.331), kind=kOutput, calls=%fused_computation.255 | convolution fusion | flops 100663296 | bytes 33579008 | tf_op jit(solution)/shard_map/dot_general | solution.py:17
  744.7 33.1 %all-reduce.4 = (f32[4096]{0:T(1024)S(1)}, f32[4096]{0:T(1024)S(1)}) all-reduce(f32[4096]{0:T(1024)S(1)} %bitcast.287, f32[4096]{0:T(1024)S(1)} %bitcast.317), channel_id=1, replica_groups=mesh['row'=4,'col'=8] {'col'}, use_global_device_ids=true, to_apply=%region_36.37 | all-reduce | flops 8192 | bytes 65536 | tf_op jit(solution)/shard_map/psum | solution.py:52
  778.9 6.3 psum.189
  785.8 5.2 all_gather.61
  795.9 5.6 all_gather.62
  804.7 1.3 convolution_bitcast_fusion
  806.0 1.3 convolution_bitcast_fusion.1
  807.3 21.0 %fusion.135 = f32[1,4096]{1,0:T(1,128)S(1)} fusion(f32[4096,2048]{0,1:T(8,128)} %subtract_subtract_fusion.1, f32[2048,1]{0,1:T(1,128)S(1)} %bitcast.332), kind=kOutput, calls=%fused_computation.256 | convolution fusion | flops 100663296 | bytes 33579008 | tf_op jit(solution)/shard_map/dot_general | solution.py:17
  828.3 33.0 %psum.190 = f32[4096]{0:T(1024)S(1)} all-reduce(f32[4096]{0:T(1024)S(1)} %bitcast.288), channel_id=1, replica_groups=mesh['row'=4,'col'=8] {'col'}, use_global_device_ids=true, to_apply=%region_40.41 | all-reduce | flops 4096 | bytes 32768 | tf_op jit(solution)/shard_map/psum | solution.py:52
  863.7 6.3 psum.191
  870.6 5.5 all_gather.63
  877.2 30.1 %fusion.11 = f32[4096,2048]{0,1:T(8,128)} fusion(f32[16384,4]{0,1:T(4,128)S(1)} %scatter.76, s32[]{:T(128)S(6)} %select_n.183, f32[16384,4]{0,1:T(4,128)S(1)} %scatter.79, s32[]{:T(128)S(6)} %select_n.184), kind=kOutput, calls=%fused_computation.39 | convolution fusion | flops 402653184 | bytes 33652744 | tf_op jit(solution)/shard_map/dot_general | solution.py:17
  907.3 41.1 %subtract_subtract_fusion = f32[4096,2048]{0,1:T(8,128)} fusion(f32[4096,2048]{0,1:T(8,128)} %subtract_subtract_fusion.1, f32[4096,2048]{0,1:T(8,128)} %fusion.11, f32[16384,4]{0,1:T(4,128)S(1)} %scatter.79, s32[]{:T(128)S(6)} %select_n.183, f32[16384,4]{0,1:T(4,128)S(1)} %scatter.76, s32[]{:T(128)S(6)} %select_n.184), kind=kOutput, calls=%fused_computation | convolution fusion | flops 419430400 | bytes 100761608 | tf_op jit(solution)/shard_map/dot_general | solution.py:17
  948.4 33.3 %copy.49 = f32[4096,2048]{1,0:T(8,128)} copy(f32[4096,2048]{0,1:T(8,128)} %subtract_subtract_fusion) | data formatting | bytes 67108864 | tf_op jit(solution)/shard_map/sub | solution.py:70
  (123 shorter events, 51.4 us)
where the time goes:
time: 991 us; the launch traced here: 982 us
  blocking collectives  472 us (48%)
  matrix products  376 us (38%)
  local copies, waits for them, and re-layouts  87.7 us (9%)
  other arithmetic  24.6 us (2%)
  between operations  22 us (2%)
    dot_general x50, matrix products, product(): jnp.dot(left, right, precision=highest, preferred_element_type=jnp.float32)  376 us
    psum x8, blocking collectives, on_device(): summed = lax.psum(product(current, vector_cols), 'col')  264 us
    psum x2, blocking collectives, from_root(): return lax.psum(kept, axis)  71.8 us
    psum x8, blocking collectives, on_device(): inner = lax.psum(jnp.sum(mapped * vector_rows), 'row')  50.2 us
    all_gather x8, blocking collectives, on_device(): whole = lax.all_gather(column, 'row', axis=0, tiled=True)  43.5 us
    all_gather x8, blocking collectives, on_device(): lax.all_gather(mapped - 0.5 * factor * inner * vector_rows, 'row', axis=0...  42.4 us
    sub x1, local copies, waits for them, and re-layouts, on_device(): current - product(reflector_rows, update_cols.T)  33.3 us
    unnamed x1, local copies, waits for them, and re-layouts  31.1 us

commit v1 on v0

--- a/solution.py
+++ b/solution.py
@@ -49,7 +49,7 @@
             vector_cols = lax.dynamic_slice_in_dim(vector, col_start, cols_local, 0)
             against_updates = product(vector, updates)
             against_reflectors = product(vector, reflectors)
-            summed = lax.psum(product(current, vector_cols), "col")
+            summed = jnp.sum(lax.all_gather(product(current, vector_cols), "col"), axis=0)
             mapped = factor * (
                 summed
                 - product(reflector_rows, against_updates)

time: 991 us -> 1060 us (1.070)
  waiting for transfers between devices: 0 us -> 141 us
  blocking collectives: 472 us -> 380 us
  between operations: 22 us -> 35.3 us
    psum x10 -> x0, blocking collectives: 336 us -> none  [the longest x8 264 us: on_device(): summed = lax.psum(product(current, vector_cols), 'col')]
    all_gather x0 -> x8, blocking collectives: none -> 244 us  [on_device(): lax.all_gather(product(current, vector_cols), 'col')]
    psum x0 -> x2, waiting for transfers between devices: none -> 141 us  [from_root(): return lax.psum(kept, axis)]
    unnamed x1 -> x13, local copies, waits for them, and re-layouts: 31.1 us -> 31.1 us
  transfers between devices with their start and end apart: 0 -> 2, of which waited for: 0 -> 2; matrix products, arithmetic and copies ran while one was open for 0% -> 0% of each run, Pallas kernels for 0% -> 0%
where the time goes in v1:
time: 1060 us; the launch traced here: 1050 us
  blocking collectives  380 us (36%)
  matrix products  376 us (35%)
  waiting for transfers between devices  141 us (13%)
  local copies, waits for them, and re-layouts  88.1 us (8%)
  between operations  35.3 us (3%)
  other arithmetic  27.3 us (3%)
    dot_general x50, matrix products, product(): jnp.dot(left, right, precision=highest, preferred_element_type=jnp.float32)  376 us
    all_gather x8, blocking collectives, on_device(): lax.all_gather(product(current, vector_cols), 'col')  244 us
    psum x2, waiting for transfers between devices, from_root(): return lax.psum(kept, axis)  141 us
    psum x8, blocking collectives, on_device(): inner = lax.psum(jnp.sum(mapped * vector_rows), 'row')  50.4 us
    all_gather x8, blocking collectives, on_device(): whole = lax.all_gather(column, 'row', axis=0, tiled=True)  43.2 us
    all_gather x8, blocking collectives, on_device(): lax.all_gather(mapped - 0.5 * factor * inner * vector_rows, 'row', axis=0...  42.1 us
    sub x1, local copies, waits for them, and re-layouts, on_device(): current - product(reflector_rows, update_cols.T)  33.3 us
    unnamed x13, local copies, waits for them, and re-layouts  31.1 us
  transfers between devices with their start and end apart: 2, of which 2 were waited for; matrix products, arithmetic and copies ran while one was open for 0% of the time, Pallas kernels for 0%

profile of v1, /device:TPU:0, one launch (start us, length us, event | category | flops | bytes accessed | tf_op | source)
XLA Modules:
  0.0 1047.9 jit_solution(17656806992550677127)
XLA Ops:
  6.5 31.1 %copy.46 = f32[4096,2048]{0,1:T(8,128)} copy(f32[4096,2048]{1,0:T(8,128)} %param.33) | data formatting | bytes 67108864 | tf_op args[0]
  37.6 1.9 broadcast_select_fusion.16
  42.4 70.3 %all-reduce.11.cloned.1.call-done = (f32[4096]{0:T(1024)}, f32[4096]{0:T(1024)}, f32[4096]{0:T(1024)}, f32[4096]{0:T(1024)}) async-done(((f32[4096]{0:T(1024)}, f32[4096]{0:T(1024)}, f32[4096]{0:T(1024)}, f32[4096]{0:T(1024)}), (f32[4096]{0:T(1024)}, f32[4096]{0:T(1024)}, f32[4096]{0:T(1024)}, f32[4096]{0:T(1024)})) %all-reduce.11.cloned.1.call-update) | async-done | bytes 65552 | tf_op jit(solution)/shard_map/psum | solution.py:13
  113.9 5.2 all_gather.96
  123.1 1.9 fusion.2
  125.2 30.7 %fusion.128 = f32[1,4096]{1,0:T(1,128)S(1)} fusion(f32[2048,1]{0,1:T(1,128)S(1)} %bitcast.328, f32[4096,2048]{1,0:T(8,128)} %param.33), kind=kOutput, calls=%fused_computation.249 | convolution fusion | flops 100663296 | bytes 33579008 | tf_op jit(solution)/shard_map/dot_general | solution.py:17
  155.9 30.6 %all-gather = f32[32768]{0:T(1024)S(1)} all-gather(f32[4096]{0:T(1024)S(1)} %bitcast.292), channel_id=2, replica_groups=mesh['row'=4,'col'=8] {'col'}, dimensions={0}, use_global_device_ids=true | all-gather | bytes 147456 | tf_op jit(solution)/shard_map/all_gather | solution.py:52
  187.9 6.3 psum.114
  194.9 5.2 all_gather.99
  201.6 5.7 all_gather.100
  211.1 1.3 convolution_bitcast_fusion.11
  212.4 1.3 convolution_bitcast_fusion.12
  213.9 30.7 %fusion.129 = f32[1,4096]{1,0:T(1,128)S(1)} fusion(f32[2048,1]{0,1:T(1,128)S(1)} %bitcast.325, f32[4096,2048]{1,0:T(8,128)} %param.33), kind=kOutput, calls=%fused_computation.250 | convolution fusion | flops 100663296 | bytes 33579008 | tf_op jit(solution)/shard_map/dot_general | solution.py:17
  245.1 30.5 %all-gather.1 = f32[32768]{0:T(1024)S(1)} all-gather(f32[4096]{0:T(1024)S(1)} %bitcast.290), channel_id=3, replica_groups=mesh['row'=4,'col'=8] {'col'}, dimensions={0}, use_global_device_ids=true | all-gather | bytes 147456 | tf_op jit(solution)/shard_map/all_gather | solution.py:52
  276.3 6.3 psum.116
  283.3 5.2 all_gather.103
  292.4 5.5 all_gather.104
  301.3 1.3 convolution_bitcast_fusion.9
  302.6 1.3 convolution_bitcast_fusion.10
  303.9 30.7 %fusion.130 = f32[1,4096]{1,0:T(1,128)S(1)} fusion(f32[2048,1]{0,1:T(1,128)S(1)} %bitcast.326, f32[4096,2048]{1,0:T(8,128)} %param.33), kind=kOutput, calls=%fused_computation.251 | convolution fusion | flops 100663296 | bytes 33579008 | tf_op jit(solution)/shard_map/dot_general | solution.py:17
  337.3 30.5 %all-gather.2 = f32[32768]{0:T(1024)S(1)} all-gather(f32[4096]{0:T(1024)S(1)} %bitcast.289), channel_id=4, replica_groups=mesh['row'=4,'col'=8] {'col'}, dimensions={0}, use_global_device_ids=true | all-gather | bytes 147456 | tf_op jit(solution)/shard_map/all_gather | solution.py:52
  368.5 6.3 psum.118
  375.5 5.2 all_gather.107
  383.4 5.5 all_gather.108
  392.2 1.3 convolution_bitcast_fusion.7
  393.5 1.3 convolution_bitcast_fusion.8
  394.9 30.7 %fusion.131 = f32[1,4096]{1,0:T(1,128)S(1)} fusion(f32[2048,1]{0,1:T(1,128)S(1)} %bitcast.327, f32[4096,2048]{1,0:T(8,128)} %param.33), kind=kOutput, calls=%fused_computation.252 | convolution fusion | flops 100663296 | bytes 33579008 | tf_op jit(solution)/shard_map/dot_general | solution.py:17
  426.1 30.5 %all-gather.3 = f32[32768]{0:T(1024)S(1)} all-gather(f32[4096]{0:T(1024)S(1)} %bitcast.291), channel_id=5, replica_groups=mesh['row'=4,'col'=8] {'col'}, dimensions={0}, use_global_device_ids=true | all-gather | bytes 147456 | tf_op jit(solution)/shard_map/all_gather | solution.py:52
  458.6 6.3 psum.119
  465.4 5.5 all_gather.111
  472.1 30.1 %fusion.14 = f32[4096,2048]{0,1:T(8,128)} fusion(f32[16384,4]{0,1:T(4,128)S(1)} %scatter.64, s32[]{:T(128)S(6)} %select_n.183, f32[16384,4]{0,1:T(4,128)S(1)} %scatter.65, s32[]{:T(128)S(6)} %select_n.184), kind=kOutput, calls=%fused_computation.58 | convolution fusion | flops 402653184 | bytes 33652744 | tf_op jit(solution)/shard_map/dot_general | solution.py:17
  502.2 41.5 %subtract_subtract_fusion.1 = f32[4096,2048]{0,1:T(8,128)} fusion(f32[4096,2048]{0,1:T(8,128)} %copy.46, f32[4096,2048]{0,1:T(8,128)} %fusion.14, f32[16384,4]{0,1:T(4,128)S(1)} %scatter.65, s32[]{:T(128)S(6)} %select_n.183, f32[16384,4]{0,1:T(4,128)S(1)} %scatter.64, s32[]{:T(128)S(6)} %select_n.184), kind=kOutput, calls=%fused_computation.1 | convolution fusion | flops 419430400 | bytes 100761608 | tf_op jit(solution)/shard_map/dot_general | solution.py:17
  543.6 1.9 broadcast_select_fusion.12
  545.6 70.5 %all-reduce.9.cloned.1.call-done = (f32[4096]{0:T(1024)}, f32[4096]{0:T(1024)}, f32[4096]{0:T(1024)}, f32[4096]{0:T(1024)}) async-done(((f32[4096]{0:T(1024)}, f32[4096]{0:T(1024)}, f32[4096]{0:T(1024)}, f32[4096]{0:T(1024)}), (f32[4096]{0:T(1024)}, f32[4096]{0:T(1024)}, f32[4096]{0:T(1024)}, f32[4096]{0:T(1024)})) %all-reduce.9.cloned.1.call-update) | async-done | bytes 65552 | tf_op jit(solution)/shard_map/psum | solution.py:13
  616.8 5.2 all_gather.112
  626.0 1.9 fusion.3
  628.1 21.2 %fusion.132 = f32[1,4096]{1,0:T(1,128)S(1)} fusion(f32[4096,2048]{0,1:T(8,128)} %subtract_subtract_fusion.1, f32[2048,1]{0,1:T(1,128)S(1)} %bitcast.332), kind=kOutput, calls=%fused_computation.253 | convolution fusion | flops 100663296 | bytes 33579008 | tf_op jit(solution)/shard_map/dot_general | solution.py:17
  649.2 30.6 %all-gather.4 = f32[32768]{0:T(1024)S(1)} all-gather(f32[4096]{0:T(1024)S(1)} %bitcast.288), channel_id=6, replica_groups=mesh['row'=4,'col'=8] {'col'}, dimensions={0}, use_global_device_ids=true | all-gather | bytes 147456 | tf_op jit(solution)/shard_map/all_gather | solution.py:52
  681.3 6.3 psum.122
  688.2 5.2 all_gather.115
  694.9 5.3 all_gather.116
  703.9 1.3 convolution_bitcast_fusion.4
  705.2 1.3 convolution_bitcast_fusion.5
  706.7 21.2 %fusion.133 = f32[1,4096]{1,0:T(1,128)S(1)} fusion(f32[4096,2048]{0,1:T(8,128)} %subtract_subtract_fusion.1, f32[2048,1]{0,1:T(1,128)S(1)} %bitcast.329), kind=kOutput, calls=%fused_computation.254 | convolution fusion | flops 100663296 | bytes 33579008 | tf_op jit(solution)/shard_map/dot_general | solution.py:17
  728.5 30.5 %all-gather.5 = f32[32768]{0:T(1024)S(1)} all-gather(f32[4096]{0:T(1024)S(1)} %bitcast.286), channel_id=7, replica_groups=mesh['row'=4,'col'=8] {'col'}, dimensions={0}, use_global_device_ids=true | all-gather | bytes 147456 | tf_op jit(solution)/shard_map/all_gather | solution.py:52
  759.7 6.3 psum.124
  766.7 5.2 all_gather.119
  775.9 5.3 all_gather.120
  784.5 1.3 convolution_bitcast_fusion.2
  785.8 1.3 convolution_bitcast_fusion.3
  787.9 21.3 %fusion.134 = f32[1,4096]{1,0:T(1,128)S(1)} fusion(f32[4096,2048]{0,1:T(8,128)} %subtract_subtract_fusion.1, f32[2048,1]{0,1:T(1,128)S(1)} %bitcast.331), kind=kOutput, calls=%fused_computation.255 | convolution fusion | flops 100663296 | bytes 33579008 | tf_op jit(solution)/shard_map/dot_general | solution.py:17
  811.1 30.5 %all-gather.6 = f32[32768]{0:T(1024)S(1)} all-gather(f32[4096]{0:T(1024)S(1)} %bitcast.285), channel_id=8, replica_groups=mesh['row'=4,'col'=8] {'col'}, dimensions={0}, use_global_device_ids=true | all-gather | bytes 147456 | tf_op jit(solution)/shard_map/all_gather | solution.py:52
  842.3 6.3 psum.126
  849.3 5.2 all_gather.123
  857.2 5.3 all_gather.124
  867.1 1.3 convolution_bitcast_fusion.1
  868.5 21.5 %fusion.135 = f32[1,4096]{1,0:T(1,128)S(1)} fusion(f32[4096,2048]{0,1:T(8,128)} %subtract_subtract_fusion.1, f32[2048,1]{0,1:T(1,128)S(1)} %bitcast.330), kind=kOutput, calls=%fused_computation.256 | convolution fusion | flops 100663296 | bytes 33579008 | tf_op jit(solution)/shard_map/dot_general | solution.py:17
  891.7 30.5 %all-gather.7 = f32[32768]{0:T(1024)S(1)} all-gather(f32[4096]{0:T(1024)S(1)} %bitcast.287), channel_id=9, replica_groups=mesh['row'=4,'col'=8] {'col'}, dimensions={0}, use_global_device_ids=true | all-gather | bytes 147456 | tf_op jit(solution)/shard_map/all_gather | solution.py:52
  922.9 6.3 psum.127
  929.8 5.2 all_gather.127
  935.0 1.3 scatter.79
  936.4 30.1 %fusion.11 = f32[4096,2048]{0,1:T(8,128)} fusion(f32[16384,4]{0,1:T(4,128)S(1)} %scatter.76, s32[]{:T(128)S(6)} %select_n.183, f32[16384,4]{0,1:T(4,128)S(1)} %scatter.79, s32[]{:T(128)S(6)} %select_n.184), kind=kOutput, calls=%fused_computation.39 | convolution fusion | flops 402653184 | bytes 33652744 | tf_op jit(solution)/shard_map/dot_general | solution.py:17
  966.5 41.0 %subtract_subtract_fusion = f32[4096,2048]{0,1:T(8,128)} fusion(f32[4096,2048]{0,1:T(8,128)} %subtract_subtract_fusion.1, f32[4096,2048]{0,1:T(8,128)} %fusion.11, f32[16384,4]{0,1:T(4,128)S(1)} %scatter.79, s32[]{:T(128)S(6)} %select_n.183, f32[16384,4]{0,1:T(4,128)S(1)} %scatter.76, s32[]{:T(128)S(6)} %select_n.184), kind=kOutput, calls=%fused_computation | convolution fusion | flops 419430400 | bytes 100761608 | tf_op jit(solution)/shard_map/dot_general | solution.py:17
  1007.5 33.3 %copy.49 = f32[4096,2048]{1,0:T(8,128)} copy(f32[4096,2048]{0,1:T(8,128)} %subtract_subtract_fusion) | data formatting | bytes 67108864 | tf_op jit(solution)/shard_map/sub | solution.py:70
  (155 shorter events, 53.4 us)
Async XLA Ops:
  6.5 106.1 %all-reduce.11.cloned.1.call-start = ((), (), s32[]{:S(2)}) async-start(), calls=%async_computation.1 | async-start | bytes 131072 | tf_op jit(solution)/shard_map/psum | solution.py:13
  39.5 576.6 %all-reduce.9.cloned.1.call-start = ((), (), s32[]{:S(2)}) async-start(), calls=%async_computation | async-start | bytes 131072 | tf_op jit(solution)/shard_map/psum | solution.py:13
  112.6 88.9 %copy-start.4 = (f32[4096]{0:T(1024)S(1)}, f32[4096]{0:T(1024)}, u32[]{:S(2)}) copy-start(f32[4096]{0:T(1024)} %get-tuple-element.202) | copy-start | bytes 49156
  125.1 167.3 %copy-start.2 = (f32[4096]{0:T(1024)S(1)}, f32[4096]{0:T(1024)}, u32[]{:S(2)}) copy-start(f32[4096]{0:T(1024)} %get-tuple-element.203) | copy-start | bytes 49156
  213.8 169.6 %copy-start = (f32[4096]{0:T(1024)S(1)}, f32[4096]{0:T(1024)}, u32[]{:S(2)}) copy-start(f32[4096]{0:T(1024)} %get-tuple-element.204) | copy-start | bytes 49156
  616.1 78.8 %copy-start.5 = (f32[4096]{0:T(1024)S(1)}, f32[4096]{0:T(1024)}, u32[]{:S(2)}) copy-start(f32[4096]{0:T(1024)} %get-tuple-element.198) | copy-start | bytes 49156
  649.2 126.6 %copy-start.3 = (f32[4096]{0:T(1024)S(1)}, f32[4096]{0:T(1024)}, u32[]{:S(2)}) copy-start(f32[4096]{0:T(1024)} %get-tuple-element.199) | copy-start | bytes 49156
  728.0 129.2 %copy-start.1 = (f32[4096]{0:T(1024)S(1)}, f32[4096]{0:T(1024)}, u32[]{:S(2)}) copy-start(f32[4096]{0:T(1024)} %get-tuple-element.200) | copy-start | bytes 49156
Sparse Core Ops, SparseCore 0:
  39.7 72.8 all-reduce.10
  545.7 70.3 all-reduce.8
